TPU v7x, 256 devices: a whole 4x4x8 slice. The times are simulated.
256 devices in a mesh: pop: 32 (over x, z), grp: 8 (over y, core).
Axes of the slice: x: 4, y: 4, z: 8, core: 2. Of those that a mesh axis runs over, the one named last changes fastest.
Arguments:
- actions: bfloat16 [131072, 1024], P(('pop', 'grp')), may hold values from -24 to 24
- elite_mask: int32 [131072], P(('pop', 'grp')), may hold values from 0 to 1, as said below
- init_state: float32 [256], replicated, may hold values from -6 to 6
- w_state: bfloat16 [256, 256], replicated, may hold values from -0.375 to 0.375
- w_action: bfloat16 [32, 256], replicated, may hold values from -1 to 1
- bias: float32 [256], replicated, may hold values from -3 to 3
- w_out: bfloat16 [256, 256], replicated, may hold values from -0.375 to 0.375
- reward_vec: float32 [256], replicated, may hold values from -0.375 to 0.375
Outputs:
- new_mean: float32 [1024], replicated
- covariance: float32 [1024, 1024], P('pop')
- returns: float32 [131072], P(('pop', 'grp'))
Inputs may be any that keep to these rules, and one draw needn't show every extreme that they name: `elite_mask`: each aligned block of 512 candidates (the candidates of one device) holds at least one elite.
All inputs are finite; a program needn't handle non-finite values.
Results may differ from a plain program's by a relative error of at most 0.0063.
Values sent between devices are 32-bit elements; how exact they have to be, the bound alone decides.
A program may use at most 64 MiB of HBM per device.

v0:
```python
import functools

import jax
import jax.numpy as jnp
from jax import lax
from jax.sharding import Mesh
from jax.sharding import PartitionSpec as P

ACT = 32
STEPS = 32
STATE = 256
POP_GRP = ("pop_0", "pop_1", "grp_0", "grp_1")
POP = ("pop_0", "pop_1")
GRP = ("grp_0", "grp_1")


def one_axis_at_a_time(array, axes):
    return functools.reduce(lax.psum, axes, array)


def sum_by_axis(subtotal, axes):
    for axis in axes:
        subtotal = lax.psum_scatter(subtotal, axis, scatter_dimension=0, tiled=True)
    return subtotal


def gathered_total(array, axis):
    pieces = lax.all_gather(array, axis)
    return pieces.sum(axis=0)


def on_device(actions, elite_mask, init_state, w_state, w_action, bias, w_out, reward_vec):
    cand_rows = actions.shape[0]
    width_all = actions.shape[1]
    weight = elite_mask.astype(jnp.float32)
    weight_b = weight.astype(jnp.bfloat16)
    local_sums = jnp.dot(weight_b[None, :], actions, preferred_element_type=jnp.float32)[0]
    local_count = jnp.sum(weight)
    sums, count = (
        one_axis_at_a_time(local_sums, POP_GRP),
        one_axis_at_a_time(local_count, POP_GRP),
    )
    new_mean = sums / count
    masked = actions * weight_b[:, None]
    pop_count = lax.axis_size(POP)
    own_rows = width_all // pop_count
    pop_index = lax.axis_index(POP)
    first_row = pop_index * own_rows
    slab = sum_by_axis(
        lax.dot_general(
            masked, actions, (((0,), (0,)), ((), ())), preferred_element_type=jnp.float32
        ),
        POP,
    )
    mine = gathered_total(slab, GRP)
    mean_rows = lax.dynamic_slice_in_dim(new_mean, first_row, own_rows, 0)
    covariance = mine / count - mean_rows[:, None] * new_mean[None, :]
    per_step = jnp.transpose(actions.reshape(cand_rows, STEPS, ACT), (1, 0, 2))
    start_state = jnp.broadcast_to(init_state[None, :], (cand_rows, STATE))

    def advance(carry, action_now):
        state, total = carry
        state_b = state.astype(jnp.bfloat16)
        pre = jnp.dot(state_b, w_state, preferred_element_type=jnp.float32)
        pre = pre + jnp.dot(action_now, w_action, preferred_element_type=jnp.float32) + bias
        hidden = jnp.tanh(pre).astype(jnp.bfloat16)
        state = 0.9 * state + jnp.dot(hidden, w_out, preferred_element_type=jnp.float32)
        total = total + jnp.sum(state * reward_vec[None, :], axis=1)
        return ((state, total), None)

    (final_state, total), unused = lax.scan(
        advance, (start_state, jnp.zeros((cand_rows,), jnp.float32)), per_step
    )
    returns = total / STEPS
    return (new_mean, covariance, returns)


def solution(mesh):
    torus = Mesh(mesh.devices.reshape(4, 8, 4, 2), ("pop_0", "pop_1", "grp_0", "grp_1"))
    placed = (P(POP_GRP, None), P(POP_GRP), P(), P(), P(), P(), P(), P())
    return jax.shard_map(
        on_device,
        mesh=torus,
        in_specs=placed,
        out_specs=(P(), P(POP, None), P(POP_GRP)),
        check_vma=False,
    )
```

profile of v0, /device:TPU:1, one launch (start us, length us, event | category | flops | bytes accessed | tf_op | source)
XLA Modules:
  0.0 195.3 jit_solution(5249627727034569487)
XLA Ops:
  7.9 4.9 %fusion.12 = f32[1024,1024]{1,0:T(8,128)} fusion(bf16[512,1024]{1,0:T(8,128)(2,1)} %param.10, bf16[512]{0:T(512)(128)(2,1)S(1)} %convert_convert_fusion), kind=kOutput, calls=%fused_computation.13 | convolution fusion | flops 1074266112 | bytes 5243904 | tf_op jit(solution)/shard_map/dot_general | solution.py:50
  12.9 53.2 %reduce-scatter.3.cloned.1.call-done = f32[256,1024]{1,0:T(8,128)} async-done(((f32[1024,1024]{1,0:T(8,128)}), f32[256,1024]{1,0:T(8,128)}) %reduce-scatter.3.cloned.1.call-update) | async-done | bytes 1048592 | tf_op jit(solution)/shard_map/reduce_scatter | solution.py:23
  66.7 35.8 %reduce-scatter.5.cloned.1.call-done = f32[32,1024]{1,0:T(8,128)} async-done(((f32[256,1024]{1,0:T(8,128)}), f32[32,1024]{1,0:T(8,128)}) %reduce-scatter.5.cloned.1.call-update) | async-done | bytes 131088 | tf_op jit(solution)/shard_map/reduce_scatter | solution.py:23
  102.8 34.1 %while.13 = (s32[]{:T(128)}, f32[512,256]{0,1:T(8,128)S(1)}, f32[512]{0:T(512)S(1)}, bf16[256,256]{1,0:T(8,128)(2,1)S(1)}, bf16[32,512,32]{1,2,0:T(8,128)(2,1)S(...) while((s32[]{:T(128)}, f32[512,256]{0,1:T(8,128)S(1)}, ...), condition=%wide.region_14.15_spmd.clone, body=%wide.region_12.14_spmd.clone.sunk | while | flops 143655424 | bytes 2943107 | solution.py:71
  103.0 0.8 multiply_reduce_fusion.2
  105.2 0.8 multiply_reduce_fusion.2
  107.3 0.8 multiply_reduce_fusion.2
  108.4 0.8 multiply_reduce_fusion.2
  109.4 0.8 multiply_reduce_fusion.2
  110.5 0.8 multiply_reduce_fusion.2
  111.6 0.8 multiply_reduce_fusion.2
  112.6 0.8 multiply_reduce_fusion.2
  113.7 0.8 multiply_reduce_fusion.2
  114.8 0.8 multiply_reduce_fusion.2
  115.8 0.8 multiply_reduce_fusion.2
  116.9 0.8 multiply_reduce_fusion.2
  118.0 0.8 multiply_reduce_fusion.2
  119.0 0.8 multiply_reduce_fusion.2
  120.1 0.8 multiply_reduce_fusion.2
  121.2 0.8 multiply_reduce_fusion.2
  122.2 0.8 multiply_reduce_fusion.2
  123.3 0.8 multiply_reduce_fusion.2
  126.5 0.8 multiply_reduce_fusion.2
  127.5 0.8 multiply_reduce_fusion.2
  132.9 0.8 multiply_reduce_fusion.2
  135.0 0.8 multiply_reduce_fusion.2
  137.7 9.1 %all-reduce.2 = (f32[1024]{0:T(1024)S(1)}, f32[]{:T(128)}) all-reduce(f32[1024]{0:T(1024)S(1)} %bitcast.28, f32[]{:T(128)} %convert_reduce_fusion), channel_id=1, replica_groups=mesh['pop_0'=4,'pop_1'=8,'grp_0'=4,'grp_1'=2] {'pop_0'}, use_global_device_ids=true, to_apply=%region_0.0 | all-reduce | flops 1025 | bytes 8200 | tf_op jit(solution)/shard_map/psum | solution.py:18
  146.8 13.1 %all-reduce = (f32[1024]{0:T(1024)S(1)}, f32[]{:T(128)}) all-reduce(f32[1024]{0:T(1024)S(1)} %get-tuple-element.112, f32[]{:T(128)} %get-tuple-element.113), channel_id=1, replica_groups=mesh['pop_0'=4,'pop_1'=8,'grp_0'=4,'grp_1'=2] {'pop_1'}, use_global_device_ids=true, to_apply=%region_1.0 | all-reduce | flops 1025 | bytes 8200 | tf_op jit(solution)/shard_map/psum | solution.py:18
  159.9 9.2 %all-reduce.1 = (f32[1024]{0:T(1024)S(1)}, f32[]{:T(128)}) all-reduce(f32[1024]{0:T(1024)S(1)} %get-tuple-element.108, f32[]{:T(128)} %get-tuple-element.109), channel_id=1, replica_groups=mesh['pop_0'=4,'pop_1'=8,'grp_0'=4,'grp_1'=2] {'grp_0'}, use_global_device_ids=true, to_apply=%region_2.0 | all-reduce | flops 1025 | bytes 8200 | tf_op jit(solution)/shard_map/psum | solution.py:18
  169.1 15.7 %all-reduce.3 = (f32[1024]{0:T(1024)S(1)}, f32[]{:T(128)}) all-reduce(f32[1024]{0:T(1024)S(1)} %get-tuple-element.110, f32[]{:T(128)} %get-tuple-element.111), channel_id=1, replica_groups=mesh['pop_0'=4,'pop_1'=8,'grp_0'=4,'grp_1'=2] {'grp_1'}, use_global_device_ids=true, to_apply=%region_3.0 | all-reduce | flops 1025 | bytes 8200 | tf_op jit(solution)/shard_map/psum | solution.py:18
  186.1 1.3 reduce_sum.28
  187.4 1.4 multiply_subtract_fusion
  (109 shorter events, 20.2 us)
Async XLA Ops:
  7.2 58.9 %reduce-scatter.3.cloned.1.call-start = ((), (), s32[]{:S(2)}) async-start(), calls=%async_computation.2 | async-start | bytes 5242880 | tf_op jit(solution)/shard_map/reduce_scatter | solution.py:23
  12.8 53.4 %copy-start = (bf16[512,1024]{1,0:T(8,128)(2,1)S(1)}, bf16[512,1024]{1,0:T(8,128)(2,1)}, u32[]{:S(2)}) copy-start(bf16[512,1024]{1,0:T(8,128)(2,1)} %param.10) | copy-start | bytes 3145732
  12.8 89.8 %copy-start.8 = (f32[256]{0:T(256)S(1)}, f32[256]{0:T(256)}, u32[]{:S(2)}) copy-start(f32[256]{0:T(256)} %param.12) | copy-start | bytes 3076
  12.8 89.9 %copy-start.1 = (bf16[256,256]{1,0:T(8,128)(2,1)S(1)}, bf16[256,256]{1,0:T(8,128)(2,1)}, u32[]{:S(2)}) copy-start(bf16[256,256]{1,0:T(8,128)(2,1)} %param.13) | copy-start | bytes 393220
  12.8 89.9 %copy-start.2 = (bf16[256,256]{1,0:T(8,128)(2,1)S(1)}, bf16[256,256]{1,0:T(8,128)(2,1)}, u32[]{:S(2)}) copy-start(bf16[256,256]{1,0:T(8,128)(2,1)} %param.16) | copy-start | bytes 393220
  12.8 89.9 %copy-start.3 = (bf16[32,256]{1,0:T(8,128)(2,1)S(1)}, bf16[32,256]{1,0:T(8,128)(2,1)}, u32[]{:S(2)}) copy-start(bf16[32,256]{1,0:T(8,128)(2,1)} %param.14) | copy-start | bytes 49156
  12.8 89.9 %copy-start.4 = (f32[256]{0:T(256)S(1)}, f32[256]{0:T(256)}, u32[]{:S(2)}) copy-start(f32[256]{0:T(256)} %param.15) | copy-start | bytes 3076
  12.8 89.9 %copy-start.5 = (f32[256]{0:T(256)S(1)}, f32[256]{0:T(256)}, u32[]{:S(2)}) copy-start(f32[256]{0:T(256)} %param.17) | copy-start | bytes 3076
  12.9 89.7 %reduce-scatter.5.cloned.1.call-start = ((), (), s32[]{:S(2)}) async-start(), calls=%async_computation.3 | async-start | bytes 1179648 | tf_op jit(solution)/shard_map/reduce_scatter | solution.py:23
  66.1 120.0 %all-gather.3.cloned.1.call-start = ((), (), s32[]{:S(2)}) async-start(), calls=%async_computation.4 | async-start | bytes 1179648 | tf_op jit(solution)/shard_map/all_gather | solution.py:28
  102.8 34.1 %copy-start.7 = (s32[512]{0:T(512)S(1)}, s32[512]{0:T(512)}, u32[]{:S(2)}) copy-start(s32[512]{0:T(512)} %param.11) | copy-start | bytes 6148
  185.5 3.3 %copy-start.6 = (f32[1024]{0:T(1024)}, f32[1024]{0:T(1024)S(1)}, u32[]{:S(2)}) copy-start(f32[1024]{0:T(1024)S(1)} %broadcast_divide_fusion) | copy-start | bytes 12292
Sparse Core Ops, SparseCore 0:
  13.0 53.0 reduce-scatter.2
  68.6 33.8 reduce-scatter.4
  104.4 29.7 all-gather.2
where the time goes:
time: 196 us; the launch traced here: 195 us
  waiting for transfers between devices  89.1 us (45%)
  blocking collectives  47.1 us (24%)
  matrix products  38.2 us (19%)
  between operations  13.9 us (7%)
  other arithmetic  5.54 us (3%)
    reduce_scatter x2, waiting for transfers between devices, sum_by_axis(): subtotal = lax.psum_scatter(subtotal, axis, scatter_dimension=0, tiled=True)  89 us
    psum x4, blocking collectives, one_axis_at_a_time(): return functools.reduce(lax.psum, axes, array)  47.1 us
    dot_general x32, matrix products, advance(): jnp.dot(hidden, w_out, preferred_element_type=jnp.float32)  24.6 us
    dot_general x32, matrix products, advance(): pre = jnp.dot(state_b, w_state, preferred_element_type=jnp.float32)  8.47 us
    dot_general x1, matrix products, on_device(): lax.dot_general(masked, actions, (((0,), (0,)), ((), ())), preferred_elem...  4.88 us
  transfers between devices with their start and end apart: 3, of which 2 were waited for; matrix products, arithmetic and copies ran while one was open for 19% of the time, Pallas kernels for 0%

commit v1 on v0

v1 whole, which is shorter than its diff:
```python
import functools

import jax
import jax.numpy as jnp
from jax import lax
from jax.experimental import pallas as pl
from jax.experimental.pallas import tpu as pltpu
from jax.sharding import Mesh
from jax.sharding import PartitionSpec as P

ACT = 32
STEPS = 32
STATE = 256
DIM = 1024
MESH = pl.DeviceIdType.MESH
AXES = ("x", "z", "y", "c")
NX, NZ, NY = 4, 8, 4
HALF = DIM // 2
PACK = 128 // ACT
FILL = (1, 2, 2, 1, 1, 1, 0)


def kernel(
    act_ref, mask_ref, init_ref, ws_ref, wa_ref, bias_ref, wo_ref, rv_ref,
    mean_ref, cov_ref, ret_ref,
    part, own, b1p, b1m, bdp, bdm, b2p, b2m, mid, c1p, c1m, cdp, cdm, c2p, c2m, low, zin, gath,
    s_c, s_x, s_y, s_z, wa_pad, state, acc,
    pair_send, pair_recv, r1_send, r1_recv, r2_send, r2_recv, z_send, z_recv, g_send, g_recv,
    sc_send, sc_recv, sx_send, sx_recv, sy_send, sy_recv, sz_send, sz_recv,
):
    x, z, y, c = (lax.axis_index(a) for a in AXES)
    sib = 1 - c
    f32, bf16 = jnp.float32, jnp.bfloat16

    def copy(src, dst, ssem, rsem, **where):
        return pltpu.make_async_remote_copy(
            src_ref=src, dst_ref=dst, send_sem=ssem, recv_sem=rsem,
            device_id=where, device_id_type=MESH,
        )

    barrier = pltpu.get_barrier_semaphore()

    def greet(**where):
        pl.semaphore_signal(barrier, inc=1, device_id=where, device_id_type=MESH)

    greet(c=sib)
    for d in range(1, NX):
        greet(x=lax.rem(x + d, NX))
    for d in range(1, NY):
        greet(y=lax.rem(y + d, NY))
        greet(y=lax.rem(y + d, NY), c=sib)
    for d in range(1, NZ):
        greet(z=lax.rem(z + d, NZ))

    wa_pad[...] = jnp.zeros_like(wa_pad)
    for j in range(PACK):
        wa_pad[j, j * ACT:(j + 1) * ACT, :] = wa_ref[...]
    state[...] = jnp.broadcast_to(init_ref[...], state.shape)
    acc[...] = jnp.zeros_like(acc)

    def rollout(first, count):
        @pl.loop(first, first + count)
        def _(g):
            block = act_ref[:, pl.ds(pl.multiple_of(g * 128, 128), 128)]
            for j in range(PACK):
                st = state[...]
                pre = jnp.dot(st.astype(bf16), ws_ref[...], preferred_element_type=f32)
                pre = pre + jnp.dot(block, wa_pad[j], preferred_element_type=f32) + bias_ref[...]
                hidden = jnp.tanh(pre).astype(bf16)
                st = 0.9 * st + jnp.dot(hidden, wo_ref[...], preferred_element_type=f32)
                state[...] = st
                acc[...] += st

    done = 0

    def fill(k):
        nonlocal done
        n = min(FILL[k], STEPS // PACK - done)
        if n > 0:
            rollout(done, n)
        done += n

    w_i = mask_ref[...]
    w_row = w_i.astype(f32)
    w_b = w_row.astype(bf16)
    sums = jnp.dot(jnp.broadcast_to(w_b, (16, w_b.shape[1])), act_ref[...], preferred_element_type=f32)
    s_c[c, 0:1, :] = sums[0:1]
    s_c[c, 1:2, :] = jnp.broadcast_to(jnp.sum(w_row, axis=1, keepdims=True), (1, DIM))

    pair = []
    side = pl.ds(pl.multiple_of(sib * HALF, HALF), HALF)
    mine = pl.ds(pl.multiple_of(c * HALF, HALF), HALF)
    for xs in range(NX):
        at = act_ref[:, xs * 256:(xs + 1) * 256].T * w_b
        prod = jnp.dot(at, act_ref[...], preferred_element_type=f32)
        part[xs] = prod.reshape(NZ, NY, 8, DIM)
        if xs == 0:
            pl.semaphore_wait(barrier, (NX - 1) + 2 * (NY - 1) + (NZ - 1) + 1)
            sc = copy(s_c.at[c], s_c.at[c], sc_send, sc_recv, c=sib)
            sc.start()
        for ys in range(NY):
            a = xs * (1 - sib) + ys * sib
            b = ys * (1 - sib) + xs * sib
            k = a * 4 + b
            cp = copy(part.at[xs, :, ys, :, side], own.at[a, b], pair_send.at[k], pair_recv.at[k], c=sib)
            cp.start()
            pair.append(cp)

    fill(0)

    def take(a, b):
        k = a * 4 + b
        copy(part.at[0, :, 0, :, side], own.at[a, b], pair_send.at[k], pair_recv.at[k], c=sib).wait_recv()
        xs = a * (1 - c) + b * c
        ys = b * (1 - c) + a * c
        own[a, b] = own[a, b] + part[xs, :, ys, :, mine]

    def all_sum(buf, n):
        total = buf[0]
        for i in range(1, n):
            total = total + buf[i]
        return total

    pos1 = x * (1 - c) + y * c
    pos2 = y * (1 - c) + x * c

    def on1(d):
        return {"x": lax.rem(x + d * (1 - c), NX), "y": lax.rem(y + d * c, NY)}

    def on2(d):
        return {"x": lax.rem(x + d * c, NX), "y": lax.rem(y + d * (1 - c), NY)}

    up1, dn1 = lax.rem(pos1 + 1, 4), lax.rem(pos1 + 3, 4)
    far1 = lax.rem(pos1 + 2, 4)
    up2, dn2 = lax.rem(pos2 + 1, 4), lax.rem(pos2 + 3, 4)
    far2 = lax.rem(pos2 + 2, 4)
    H0, H1 = pl.ds(0, 4), pl.ds(4, 4)

    for b in range(4):
        take(far1, b)
    m1p = copy(own.at[far1, :, H0], b1p, r1_send.at[0], r1_recv.at[0], **on1(1))
    m1m = copy(own.at[far1, :, H1], b1m, r1_send.at[1], r1_recv.at[1], **on1(3))
    m1p.start()
    m1m.start()
    for b in range(4):
        take(up1, b)
    mdp = copy(own.at[up1, :, H1], bdp, r1_send.at[2], r1_recv.at[2], **on1(1))
    mdp.start()
    for b in range(4):
        take(dn1, b)
    mdm = copy(own.at[dn1, :, H0], bdm, r1_send.at[3], r1_recv.at[3], **on1(3))
    mdm.start()
    for b in range(4):
        take(pos1, b)
    sc.wait_recv()
    s_x[x] = all_sum(s_c, 2)
    sx = []
    for d in range(1, NX):
        cp = copy(s_x.at[x], s_x.at[x], sx_send.at[d], sx_recv.at[d], x=lax.rem(x + d, NX))
        cp.start()
        sx.append(cp)

    fill(1)

    m1p.wait_recv()
    own[up1, :, H0] = own[up1, :, H0] + b1p[...]
    m2p = copy(own.at[up1, :, H0], b2p, r1_send.at[4], r1_recv.at[4], **on1(1))
    m2p.start()
    m1m.wait_recv()
    own[dn1, :, H1] = own[dn1, :, H1] + b1m[...]
    m2m = copy(own.at[dn1, :, H1], b2m, r1_send.at[5], r1_recv.at[5], **on1(3))
    m2m.start()

    for cp in sx:
        cp.wait_recv()
    s_y[y] = all_sum(s_x, NX)
    sy = []
    for d in range(1, NY):
        cp = copy(s_y.at[y], s_y.at[y], sy_send.at[d], sy_recv.at[d], y=lax.rem(y + d, NY))
        cp.start()
        sy.append(cp)

    fill(2)

    mdm.wait_recv()
    mdp.wait_recv()
    m2p.wait_recv()
    mid[:, H0] = own[pos1, :, H0] + b2p[...] + bdm[...]
    m2m.wait_recv()
    mid[:, H1] = own[pos1, :, H1] + b2m[...] + bdp[...]

    n1p = copy(mid.at[far2, H0], c1p, r2_send.at[0], r2_recv.at[0], **on2(1))
    n1m = copy(mid.at[far2, H1], c1m, r2_send.at[1], r2_recv.at[1], **on2(3))
    ndp = copy(mid.at[up2, H1], cdp, r2_send.at[2], r2_recv.at[2], **on2(1))
    ndm = copy(mid.at[dn2, H0], cdm, r2_send.at[3], r2_recv.at[3], **on2(3))
    for cp in (n1p, n1m, ndp, ndm):
        cp.start()

    for cp in sy:
        cp.wait_recv()
    s_z[z] = all_sum(s_y, NY)
    sz = []
    for d in range(1, NZ):
        cp = copy(s_z.at[z], s_z.at[z], sz_send.at[d], sz_recv.at[d], z=lax.rem(z + d, NZ))
        cp.start()
        sz.append(cp)

    fill(3)

    n1p.wait_recv()
    mid[up2, H0] = mid[up2, H0] + c1p[...]
    n2p = copy(mid.at[up2, H0], c2p, r2_send.at[4], r2_recv.at[4], **on2(1))
    n2p.start()
    n1m.wait_recv()
    mid[dn2, H1] = mid[dn2, H1] + c1m[...]
    n2m = copy(mid.at[dn2, H1], c2m, r2_send.at[5], r2_recv.at[5], **on2(3))
    n2m.start()

    fill(4)

    ndm.wait_recv()
    ndp.wait_recv()
    n2p.wait_recv()
    low[H0] = mid[pos2, H0] + c2p[...] + cdm[...]
    n2m.wait_recv()
    low[H1] = mid[pos2, H1] + c2m[...] + cdp[...]

    zs = []
    for d in range(1, NZ):
        to = lax.rem(z + d, NZ)
        cp = copy(low.at[to], zin.at[z], z_send.at[d], z_recv.at[d], z=to)
        cp.start()
        zs.append(cp)
    zin[z] = low[z]

    fill(5)

    for cp in sz:
        cp.wait_recv()
    total = all_sum(s_z, NZ)
    count = total[1:2]
    mean = total[0:1] / count
    mean_ref[...] = mean
    base = x * 256 + z * 32 + y * 8
    lane = lax.broadcasted_iota(jnp.int32, (8, DIM), 1)
    row = lax.broadcasted_iota(jnp.int32, (8, DIM), 0)
    mean_col = jnp.sum(jnp.where(lane == base + row, jnp.broadcast_to(mean, (8, DIM)), 0.0), axis=1, keepdims=True)
    outer = mean_col * mean
    cov_ref[0:8, :] = outer

    for cp in zs:
        cp.wait_recv()
    second = all_sum(zin, NZ)
    gath[y, c] = second / count[:, 0:1] - cov_ref[0:8, mine]
    gs = []
    k = 0
    for dy in range(NY):
        for dc in range(2):
            if dy + dc == 0:
                continue
            cp = copy(
                gath.at[y, c], gath.at[y, c], g_send.at[k], g_recv.at[k],
                y=lax.rem(y + dy, NY), c=(sib if dc else c),
            )
            cp.start()
            gs.append(cp)
            k += 1

    fill(6)
    rollout(done, STEPS // PACK - done) if done < STEPS // PACK else None
    scaled = acc[...] * (rv_ref[...] * (1.0 / STEPS))
    folded = scaled[:, :128] + scaled[:, 128:]
    ret_ref[...] = jnp.sum(folded.T, axis=0, keepdims=True)

    for cp in gs:
        cp.wait_recv()
    for ys in range(NY):
        for cc in range(2):
            cov_ref[ys * 8:(ys + 1) * 8, cc * HALF:(cc + 1) * HALF] = gath[ys, cc]

    for cp in pair + [sc, m1p, m1m, mdp, mdm, m2p, m2m, n1p, n1m, ndp, ndm, n2p, n2m] + sx + sy + sz + zs + gs:
        cp.wait_send()


def on_device(actions, elite_mask, init_state, w_state, w_action, bias, w_out, reward_vec):
    cand = actions.shape[0]
    f32 = jnp.float32
    vmem = pl.BlockSpec(memory_space=pltpu.VMEM)
    dma = pltpu.SemaphoreType.DMA
    V = pltpu.VMEM
    big = (4, 4, 8, HALF)
    small = (4, 8, HALF)
    scratch = (
        [V((NX, NZ, NY, 8, DIM), f32), V((4, 4, NZ, 8, HALF), f32)]
        + [V(big, f32)] * 6
        + [V((4, NZ, 8, HALF), f32)]
        + [V(small, f32)] * 6
        + [V((NZ, 8, HALF), f32), V((NZ, 8, HALF), f32), V((NY, 2, 8, HALF), f32)]
        + [V((n, 2, DIM), f32) for n in (2, NX, NY, NZ)]
        + [V((PACK, 128, STATE), jnp.bfloat16), V((cand, STATE), f32), V((cand, STATE), f32)]
        + [dma((16,)), dma((16,)), dma((6,)), dma((6,)), dma((6,)), dma((6,)), dma((NZ,)), dma((NZ,)), dma((7,)), dma((7,))]
        + [dma(()), dma(()), dma((NX,)), dma((NX,)), dma((NY,)), dma((NY,)), dma((NZ,)), dma((NZ,))]
    )
    mean, cov, ret = pl.pallas_call(
        kernel,
        out_shape=(
            jax.ShapeDtypeStruct((1, DIM), f32),
            jax.ShapeDtypeStruct((32, DIM), f32),
            jax.ShapeDtypeStruct((1, cand), f32),
        ),
        in_specs=[vmem] * 8,
        out_specs=[vmem] * 3,
        scratch_shapes=scratch,
        compiler_params=pltpu.CompilerParams(collective_id=0, has_side_effects=True, vmem_limit_bytes=48 * 1024 * 1024),
    )(
        actions, elite_mask.reshape(1, cand), init_state.reshape(1, STATE), w_state, w_action,
        bias.reshape(1, STATE), w_out, reward_vec.reshape(1, STATE),
    )
    return mean.reshape(DIM), cov, ret.reshape(cand)


def solution(mesh):
    torus = Mesh(mesh.devices.reshape(NX, NZ, NY, 2), AXES)
    placed = (P(AXES, None), P(AXES), P(), P(), P(), P(), P(), P())
    return jax.shard_map(
        on_device,
        mesh=torus,
        in_specs=placed,
        out_specs=(P(), P(("x", "z"), None), P(AXES)),
        check_vma=False,
    )
```

time: 196 us -> 51.2 us (0.26)
  waiting for transfers between devices: 89.1 us -> 0 us
  blocking collectives: 47.1 us -> 0 us
  Pallas kernels: 0 us -> 44 us
  matrix products: 38.2 us -> 0 us
  between operations: 13.9 us -> 0.68 us
  other arithmetic: 5.54 us -> 0 us
  local copies, waits for them, and re-layouts: 0.77 us -> 6.27 us
    reduce_scatter x2 -> x0, waiting for transfers between devices: 89 us -> none  [sum_by_axis(): subtotal = lax.psum_scatter(subtotal, axis, scatter_dimension=0, tiled=True)]
    psum x4 -> x0, blocking collectives: 47.1 us -> none  [one_axis_at_a_time(): return functools.reduce(lax.psum, axes, array)]
    pallas_call x0 -> x1, Pallas kernels: none -> 44 us  [on_device(): pl.pallas_call(kernel, out_shape=(jax.ShapeDtypeStruct((1, DIM), f32), ja...]
    dot_general x66 -> x0, matrix products: 38.2 us -> none  [the longest x32 24.6 us: advance(): jnp.dot(hidden, w_out, preferred_element_type=jnp.float32)]
    unnamed x19, local copies, waits for them, and re-layouts: 0.59 us -> 6.27 us
  transfers between devices with their start and end apart: 3 -> 0, of which waited for: 2 -> 0; matrix products, arithmetic and copies ran while one was open for 19% -> 0% of each run, Pallas kernels for 0% -> 0%
where the time goes in v1:
time: 51.2 us; the launch traced here: 51 us
  Pallas kernels  44 us (86%)
  local copies, waits for them, and re-layouts  6.27 us (12%)
  between operations  0.68 us (1%)
    pallas_call x1, Pallas kernels, on_device(): pl.pallas_call(kernel, out_shape=(jax.ShapeDtypeStruct((1, DIM), f32), ja...  44 us
    unnamed x19, local copies, waits for them, and re-layouts  6.27 us

profile of v1, /device:TPU:1, one launch (start us, length us, event | category | flops | bytes accessed | tf_op | source)
XLA Modules:
  0.0 51.0 jit_solution(16397454546000809814)
XLA Ops:
  0.6 0.0 copy-start.6
  0.6 0.0 copy-start.7
  0.7 0.0 copy-start.4
  0.7 0.0 copy-start.5
  0.7 0.6 %copy-done.6 = f32[256]{0:T(256)S(1)} copy-done((f32[256]{0:T(256)S(1)}, f32[256]{0:T(256)}, u32[]{:S(2)}) %copy-start.6) | copy-done | bytes 1048
  1.3 0.0 copy-done.7
  1.3 0.0 copy-done.4
  1.3 0.0 copy-done.5
  1.4 0.0 copy-start
  1.4 1.2 %copy-done = bf16[512,1024]{1,0:T(8,128)(2,1)S(1)} copy-done((bf16[512,1024]{1,0:T(8,128)(2,1)S(1)}, bf16[512,1024]{1,0:T(8,128)(2,1)}, u32[]{:S(2)}) %copy-start) | copy-done | bytes 1048600
  2.6 0.0 copy-start.1
  2.6 0.9 %copy-done.1 = bf16[256,256]{1,0:T(8,128)(2,1)S(1)} copy-done((bf16[256,256]{1,0:T(8,128)(2,1)S(1)}, bf16[256,256]{1,0:T(8,128)(2,1)}, u32[]{:S(2)}) %copy-start.1) | copy-done | bytes 131096
  3.5 0.0 copy-start.2
  3.5 0.9 %copy-done.2 = bf16[256,256]{1,0:T(8,128)(2,1)S(1)} copy-done((bf16[256,256]{1,0:T(8,128)(2,1)S(1)}, bf16[256,256]{1,0:T(8,128)(2,1)}, u32[]{:S(2)}) %copy-start.2) | copy-done | bytes 131096
  4.4 0.0 copy-start.3
  4.4 0.7 %copy-done.3 = bf16[32,256]{1,0:T(8,128)(2,1)S(1)} copy-done((bf16[32,256]{1,0:T(8,128)(2,1)S(1)}, bf16[32,256]{1,0:T(8,128)(2,1)}, u32[]{:S(2)}) %copy-start.3) | copy-done | bytes 16408
  5.1 44.0 %shard_map.103 = (f32[1,1024]{1,0:T(1,128)S(1)}, f32[32,1024]{1,0:T(8,128)S(1)}, f32[1,512]{1,0:T(1,128)S(1)}) custom-call(bf16[512,1024]{1,0:T(8,128)(2,1)S(1)} %copy-done, s32[1,512]{1,0:T(1,128)S(1)} %bitcast.7, f32[1,256]{1,0:T(1,128)S(1)} %bitcast.9, bf16[256,256]{1,0:T(8,128)(2,1)S(1)} %copy-done.1, bf16[32,256]{1,0:T(8,128)(2,1)S(1)} %copy-done.3, ...), custom_call_target="tpu_custom_call" | custom-call | tf_op jit(solution)/shard_map/pallas_call | solution.py:304
  49.1 0.6 %copy.14 = f32[1024]{0:T(1024)} copy(f32[1024]{0:T(1024)S(1)} %bitcast.6) | data formatting | bytes 8192
  49.7 0.7 %copy.15 = f32[32,1024]{1,0:T(8,128)} copy(f32[32,1024]{1,0:T(8,128)S(1)} %get-tuple-element.13) | data formatting | bytes 262144
  50.4 0.6 %copy.16 = f32[512]{0:T(512)} copy(f32[512]{0:T(512)S(1)} %bitcast.8) | data formatting | bytes 4096
Async XLA Ops:
  0.6 0.7 %copy-start.6 = (f32[256]{0:T(256)S(1)}, f32[256]{0:T(256)}, u32[]{:S(2)}) copy-start(f32[256]{0:T(256)} %param.13) | copy-start | bytes 3076
  0.6 0.7 %copy-start.7 = (f32[256]{0:T(256)S(1)}, f32[256]{0:T(256)}, u32[]{:S(2)}) copy-start(f32[256]{0:T(256)} %param.15) | copy-start | bytes 3076
  0.7 0.7 %copy-start.4 = (s32[512]{0:T(512)S(1)}, s32[512]{0:T(512)}, u32[]{:S(2)}) copy-start(s32[512]{0:T(512)} %param.9) | copy-start | bytes 6148
  0.7 0.7 %copy-start.5 = (f32[256]{0:T(256)S(1)}, f32[256]{0:T(256)}, u32[]{:S(2)}) copy-start(f32[256]{0:T(256)} %param.10) | copy-start | bytes 3076
  1.4 1.2 %copy-start = (bf16[512,1024]{1,0:T(8,128)(2,1)S(1)}, bf16[512,1024]{1,0:T(8,128)(2,1)}, u32[]{:S(2)}) copy-start(bf16[512,1024]{1,0:T(8,128)(2,1)} %act_ref.1) | copy-start | bytes 3145732
  2.6 0.9 %copy-start.1 = (bf16[256,256]{1,0:T(8,128)(2,1)S(1)}, bf16[256,256]{1,0:T(8,128)(2,1)}, u32[]{:S(2)}) copy-start(bf16[256,256]{1,0:T(8,128)(2,1)} %ws_ref.1) | copy-start | bytes 393220
  3.5 0.9 %copy-start.2 = (bf16[256,256]{1,0:T(8,128)(2,1)S(1)}, bf16[256,256]{1,0:T(8,128)(2,1)}, u32[]{:S(2)}) copy-start(bf16[256,256]{1,0:T(8,128)(2,1)} %wo_ref.1) | copy-start | bytes 393220
  4.4 0.7 %copy-start.3 = (bf16[32,256]{1,0:T(8,128)(2,1)S(1)}, bf16[32,256]{1,0:T(8,128)(2,1)}, u32[]{:S(2)}) copy-start(bf16[32,256]{1,0:T(8,128)(2,1)} %wa_ref.1) | copy-start | bytes 49156

commit v2 on v0

v2 whole, which is shorter than its diff:
```python
import jax
import jax.numpy as jnp
from jax import lax
from jax.experimental import pallas as pl
from jax.experimental.pallas import tpu as pltpu
from jax.sharding import Mesh
from jax.sharding import PartitionSpec as P

ACT = 32
STEPS = 32
STATE = 256
DIM = 1024
MESH = pl.DeviceIdType.MESH
AXES = ("x", "z", "y", "c")
NX, NZ, NY = 4, 8, 4
PACK = 128 // ACT
FILL = (3, 10, 9, 4, 4, 2)


def kernel(
    act_hbm, mask_hbm, init_hbm, ws_hbm, wa_hbm, bias_hbm, wo_hbm, rv_hbm,
    mean_ref, cov_ref, ret_ref,
    act, mask, init, ws, wa, bias, wo, rv,
    at, part, own, b1p, b1m, bdp, bdm, b2p, b2m, mid, c1p, c1m, cdp, cdm, c2p, c2m, low, zin, gath,
    s_c, s_x, s_y, s_z, wa_pad, state, acc,
    load_sem, hello,
    pair_send, pair_recv, r1_send, r1_recv, r2_send, r2_recv, z_send, z_recv, g_send, g_recv,
    sc_send, sc_recv, sx_send, sx_recv, sy_send, sy_recv, sz_send, sz_recv,
):
    x, z, y, c = (lax.axis_index(a) for a in AXES)
    sib = 1 - c
    f32, bf16 = jnp.float32, jnp.bfloat16

    def at_x(d):
        return {"x": lax.rem(x + d, NX)}

    def at_y(d):
        return {"y": lax.rem(y + d, NY)}

    def at_z(d):
        return {"z": lax.rem(z + d, NZ)}

    def copy(src, dst, ssem, rsem, where):
        return pltpu.make_async_remote_copy(
            src_ref=src, dst_ref=dst, send_sem=ssem, recv_sem=rsem,
            device_id=where, device_id_type=MESH,
        )

    def signal(sem, where):
        pl.semaphore_signal(sem, inc=1, device_id=where, device_id_type=MESH)

    near = [{"c": sib}, at_x(1), at_x(3), at_y(1), at_y(3), at_z(1), at_z(NZ - 1)]
    barrier = pltpu.get_barrier_semaphore()
    for where in near:
        signal(barrier, where)

    rows = act_hbm.shape[0] // 4
    loads = [
        pltpu.make_async_copy(act_hbm.at[pl.ds(i * rows, rows)], act.at[pl.ds(i * rows, rows)], load_sem.at[i])
        for i in range(4)
    ]
    for i, (src, dst) in enumerate((
        (mask_hbm, mask), (init_hbm, init), (ws_hbm, ws), (wa_hbm, wa), (bias_hbm, bias), (wo_hbm, wo), (rv_hbm, rv)
    )):
        loads.append(pltpu.make_async_copy(src, dst, load_sem.at[4 + i]))
    for cp in loads:
        cp.start()
    for cp in loads[:5]:
        cp.wait()

    w_row = mask[...].astype(f32)
    w_b = w_row.astype(bf16)
    for xs in range(NX):
        at[xs * 256:(xs + 1) * 256, :] = act[:, xs * 256:(xs + 1) * 256].T * w_b

    pos1 = x * (1 - c) + y * c
    pos2 = y * (1 - c) + x * c
    sib1 = y * (1 - c) + x * c

    def on1(d):
        return {"x": lax.rem(x + d * (1 - c), NX), "y": lax.rem(y + d * c, NY)}

    def on2(d):
        return {"x": lax.rem(x + d * c, NX), "y": lax.rem(y + d * (1 - c), NY)}

    def ring(pos):
        return lax.rem(pos + 1, 4), lax.rem(pos + 2, 4), lax.rem(pos + 3, 4)

    up1, far1, dn1 = ring(pos1)
    up2, far2, dn2 = ring(pos2)
    far_sib = lax.rem(sib1 + 2, 4)

    def product(core, pair):
        for i in range(4):
            xs = (2 * pair + i // 2) * (1 - core) + i * core
            half = (i % 2) * (1 - core) + pair * core
            left = at[pl.ds(pl.multiple_of(xs * 256, 256), 256), :]
            right = act[:, pl.ds(pl.multiple_of(core * 512 + half * 256, 256), 256)]
            prod = jnp.dot(left, right, preferred_element_type=f32)
            for k in range(2):
                part[core, xs, 2 * half + k] = prod[:, k * 128:(k + 1) * 128]

    def pair_copy(core, a, b):
        xs = a * (1 - core) + b * core
        ys = b * (1 - core) + a * core
        return copy(part.at[core, xs, ys], own.at[a, b], pair_send.at[a * 4 + b], pair_recv.at[a * 4 + b], {"c": sib})

    def give(a):
        for b in range(4):
            cp = pair_copy(sib, a, b)
            cp.start()

    def other(a):
        return a + 1 - 2 * lax.rem(a, 2)

    pair_sib = lax.div(far_sib, 2)
    pair_own = lax.div(far1, 2)
    product(sib, pair_sib)
    pl.semaphore_wait(barrier, len(near))
    give(far_sib)
    give(other(far_sib))
    for where in near:
        signal(hello.at[0], where)

    sums = jnp.dot(jnp.broadcast_to(w_b, (16, w_b.shape[1])), act[...], preferred_element_type=f32)
    s_c[c, 0:1, :] = sums[0:1]
    s_c[c, 1:2, :] = jnp.broadcast_to(jnp.sum(w_row, axis=1, keepdims=True), (1, DIM))
    sc = copy(s_c.at[c], s_c.at[c], sc_send, sc_recv, {"c": sib})
    sc.start()

    product(c, pair_own)
    product(sib, 1 - pair_sib)
    give(lax.rem(far_sib + 2, 4))
    give(other(lax.rem(far_sib + 2, 4)))
    product(c, 1 - pair_own)

    for cp in loads[5:]:
        cp.wait()
    wa_pad[...] = jnp.zeros_like(wa_pad)
    for j in range(PACK):
        wa_pad[j, j * ACT:(j + 1) * ACT, :] = wa[...]
    state[...] = jnp.broadcast_to(init[...], state.shape)
    acc[...] = jnp.zeros_like(acc)
    done = 0

    def fill(k):
        nonlocal done
        count = min(FILL[k], STEPS - done) if k < len(FILL) else STEPS - done
        if count <= 0:
            return

        @pl.loop(done, done + count)
        def _(t):
            block = act[:, pl.ds(pl.multiple_of(lax.div(t, PACK) * 128, 128), 128)]
            st = state[...]
            pre = jnp.dot(st.astype(bf16), ws[...], preferred_element_type=f32)
            pre = pre + jnp.dot(block, wa_pad[lax.rem(t, PACK)], preferred_element_type=f32) + bias[...]
            hidden = jnp.tanh(pre).astype(bf16)
            st = 0.9 * st + jnp.dot(hidden, wo[...], preferred_element_type=f32)
            state[...] = st
            acc[...] += st

        done += count

    def take(a):
        for b in range(4):
            pair_copy(c, a, b).wait_recv()
            xs = a * (1 - c) + b * c
            ys = b * (1 - c) + a * c
            own[a, b] = own[a, b] + part[c, xs, ys]

    def all_sum(buf, n):
        total = buf[0]
        for i in range(1, n):
            total = total + buf[i]
        return total

    def spread(buf, pos, n, ssem, rsem, to):
        cps = []
        for d in range(1, n):
            cp = copy(buf.at[pos], buf.at[pos], ssem.at[d], rsem.at[d], to(d))
            cp.start()
            cps.append(cp)
        return cps

    H0, H1 = pl.ds(0, 128), pl.ds(128, 128)

    sc.wait_recv()
    s_x[x] = all_sum(s_c, 2)
    pl.semaphore_wait(hello.at[0], len(near))
    sx = spread(s_x, x, NX, sx_send, sx_recv, at_x)
    for where in near[3:]:
        signal(hello.at[1], where)

    take(far1)
    m1p = copy(own.at[far1, :, H0], b1p, r1_send.at[0], r1_recv.at[0], on1(1))
    m1m = copy(own.at[far1, :, H1], b1m, r1_send.at[1], r1_recv.at[1], on1(3))
    m1p.start()
    m1m.start()
    fill(0)
    take(other(far1))
    take(lax.rem(other(far1) + 2, 4))
    mdp = copy(own.at[up1, :, H1], bdp, r1_send.at[2], r1_recv.at[2], on1(1))
    mdm = copy(own.at[dn1, :, H0], bdm, r1_send.at[3], r1_recv.at[3], on1(3))
    mdp.start()
    mdm.start()
    take(pos1)

    fill(1)

    m1p.wait_recv()
    own[up1, :, H0] = own[up1, :, H0] + b1p[...]
    m2p = copy(own.at[up1, :, H0], b2p, r1_send.at[4], r1_recv.at[4], on1(1))
    m2p.start()
    m1m.wait_recv()
    own[dn1, :, H1] = own[dn1, :, H1] + b1m[...]
    m2m = copy(own.at[dn1, :, H1], b2m, r1_send.at[5], r1_recv.at[5], on1(3))
    m2m.start()

    pl.semaphore_wait(hello.at[1], 4)
    for where in near[3:]:
        signal(hello.at[2], where)
    fill(2)

    for cp in sx:
        cp.wait_recv()
    s_y[y] = all_sum(s_x, NX)

    mdm.wait_recv()
    mdp.wait_recv()
    m2p.wait_recv()
    mid[:, H0] = own[pos1, :, H0] + b2p[...] + bdm[...]
    n1p = copy(mid.at[far2, H0], c1p, r2_send.at[0], r2_recv.at[0], on2(1))
    n1p.start()
    m2m.wait_recv()
    mid[:, H1] = own[pos1, :, H1] + b2m[...] + bdp[...]
    n1m = copy(mid.at[far2, H1], c1m, r2_send.at[1], r2_recv.at[1], on2(3))
    n1m.start()
    sy = spread(s_y, y, NY, sy_send, sy_recv, at_y)
    ndp = copy(mid.at[up2, H1], cdp, r2_send.at[2], r2_recv.at[2], on2(1))
    ndm = copy(mid.at[dn2, H0], cdm, r2_send.at[3], r2_recv.at[3], on2(3))
    ndp.start()
    ndm.start()

    fill(3)

    n1p.wait_recv()
    mid[up2, H0] = mid[up2, H0] + c1p[...]
    n2p = copy(mid.at[up2, H0], c2p, r2_send.at[4], r2_recv.at[4], on2(1))
    n2p.start()
    n1m.wait_recv()
    mid[dn2, H1] = mid[dn2, H1] + c1m[...]
    n2m = copy(mid.at[dn2, H1], c2m, r2_send.at[5], r2_recv.at[5], on2(3))
    n2m.start()

    for cp in sy:
        cp.wait_recv()
    s_z[z] = all_sum(s_y, NY)
    pl.semaphore_wait(hello.at[2], 4)
    sz = spread(s_z, z, NZ, sz_send, sz_recv, at_z)

    fill(4)

    ndm.wait_recv()
    ndp.wait_recv()
    n2p.wait_recv()
    low[H0] = mid[pos2, H0] + c2p[...] + cdm[...]
    n2m.wait_recv()
    low[H1] = mid[pos2, H1] + c2m[...] + cdp[...]

    zs = []
    for d in (4, 3, 5, 2, 6, 1, 7):
        to = lax.rem(z + d, NZ)
        src = low.at[pl.ds(pl.multiple_of(to * 32, 32), 32)]
        cp = copy(src, zin.at[z], z_send.at[d], z_recv.at[d], {"z": to})
        cp.start()
        zs.append(cp)
    zin[z] = low[pl.ds(pl.multiple_of(z * 32, 32), 32), :]

    fill(5)

    for cp in sz:
        cp.wait_recv()
    total = all_sum(s_z, NZ)
    count = total[1:2]
    mean = total[0:1] / count
    mean_ref[...] = mean
    lane = lax.broadcasted_iota(jnp.int32, (32, DIM), 1)
    row = lax.broadcasted_iota(jnp.int32, (32, DIM), 0) + (x * 256 + z * 32)
    mean_col = jnp.sum(jnp.where(lane == row, jnp.broadcast_to(mean, (32, DIM)), 0.0), axis=1, keepdims=True)
    outer = mean_col * mean_ref[:, pl.ds(pl.multiple_of(c * 512 + y * 128, 128), 128)]

    for cp in zs:
        cp.wait_recv()
    gath[y, c] = all_sum(zin, NZ) / count[:, 0:1] - outer
    gs = []
    for k, (dy, dc) in enumerate(((2, 0), (2, 1), (1, 0), (1, 1), (3, 0), (3, 1), (0, 1))):
        where = {"y": lax.rem(y + dy, NY), "c": sib if dc else c}
        cp = copy(gath.at[y, c], gath.at[y, c], g_send.at[k], g_recv.at[k], where)
        cp.start()
        gs.append(cp)

    fill(6)
    scaled = acc[...] * (rv[...] * (1.0 / STEPS))
    folded = scaled[:, :128] + scaled[:, 128:]
    ret_ref[...] = jnp.sum(folded.T, axis=0, keepdims=True)

    for a in range(4):
        for b in range(4):
            pair_copy(sib, a, b).wait_send()
    for cp in [sc, m1p, m1m, mdp, mdm, m2p, m2m, n1p, n1m, ndp, ndm, n2p, n2m] + sx + sy + sz + zs:
        cp.wait_send()
    for cp in gs:
        cp.wait_recv()
    for ys in range(NY):
        for cc in range(2):
            cov_ref[:, cc * 512 + ys * 128:cc * 512 + (ys + 1) * 128] = gath[ys, cc]
    for cp in gs:
        cp.wait_send()


def write_out(mean, cov, ret, mean_hbm, cov_hbm, ret_hbm, sem):
    cps = [
        pltpu.make_async_copy(src, dst, sem.at[i])
        for i, (src, dst) in enumerate(((cov, cov_hbm), (mean, mean_hbm), (ret, ret_hbm)))
    ]
    for cp in cps:
        cp.start()
    for cp in cps:
        cp.wait()


def on_device(actions, elite_mask, init_state, w_state, w_action, bias, w_out, reward_vec):
    cand = actions.shape[0]
    f32, i32, bf16 = jnp.float32, jnp.int32, jnp.bfloat16
    vmem = pl.BlockSpec(memory_space=pltpu.VMEM)
    hbm = pl.BlockSpec(memory_space=pltpu.HBM)
    dma = pltpu.SemaphoreType.DMA
    V = pltpu.VMEM
    scratch = (
        [V((cand, DIM), bf16), V((1, cand), i32), V((1, STATE), f32), V((STATE, STATE), bf16), V((ACT, STATE), bf16)]
        + [V((1, STATE), f32), V((STATE, STATE), bf16), V((1, STATE), f32)]
        + [V((DIM, cand), bf16), V((2, 4, 4, 256, 128), f32), V((4, 4, 256, 128), f32)]
        + [V((4, 128, 128), f32)] * 6
        + [V((4, 256, 128), f32)]
        + [V((128, 128), f32)] * 6
        + [V((256, 128), f32), V((NZ, 32, 128), f32), V((NY, 2, 32, 128), f32)]
        + [V((n, 2, DIM), f32) for n in (2, NX, NY, NZ)]
        + [V((PACK, 128, STATE), bf16), V((cand, STATE), f32), V((cand, STATE), f32)]
        + [dma((11,)), pltpu.SemaphoreType.REGULAR((3,))]
        + [dma((16,)), dma((16,)), dma((6,)), dma((6,)), dma((6,)), dma((6,)), dma((NZ,)), dma((NZ,)), dma((7,)), dma((7,))]
        + [dma(()), dma(()), dma((NX,)), dma((NX,)), dma((NY,)), dma((NY,)), dma((NZ,)), dma((NZ,))]
    )
    shapes = (
        jax.ShapeDtypeStruct((1, DIM), f32),
        jax.ShapeDtypeStruct((32, DIM), f32),
        jax.ShapeDtypeStruct((1, cand), f32),
    )
    args = (
        actions, elite_mask.reshape(1, cand), init_state.reshape(1, STATE), w_state, w_action,
        bias.reshape(1, STATE), w_out, reward_vec.reshape(1, STATE),
    )
    found = pl.pallas_call(
        kernel,
        out_shape=shapes,
        in_specs=[hbm] * 8,
        out_specs=[vmem] * 3,
        scratch_shapes=scratch,
        compiler_params=pltpu.CompilerParams(collective_id=0, has_side_effects=True, vmem_limit_bytes=48 * 1024 * 1024),
    )(*(pltpu.with_memory_space_constraint(a, pltpu.HBM) for a in args))
    mean, cov, ret = pl.pallas_call(
        write_out, out_shape=shapes, in_specs=[vmem] * 3, out_specs=[hbm] * 3, scratch_shapes=[dma((3,))],
        compiler_params=pltpu.CompilerParams(vmem_limit_bytes=1024 * 1024),
    )(*found)
    return mean.reshape(DIM), cov, ret.reshape(cand)


def solution(mesh):
    torus = Mesh(mesh.devices.reshape(NX, NZ, NY, 2), AXES)
    placed = (P(AXES, None), P(AXES), P(), P(), P(), P(), P(), P())
    return jax.shard_map(
        on_device,
        mesh=torus,
        in_specs=placed,
        out_specs=(P(), P(("x", "z"), None), P(AXES)),
        check_vma=False,
    )
```

time: 196 us -> 43.2 us (0.22)
  waiting for transfers between devices: 89.1 us -> 0 us
  blocking collectives: 47.1 us -> 0 us
  Pallas kernels: 0 us -> 42.5 us
  matrix products: 38.2 us -> 0 us
  between operations: 13.9 us -> 0.64 us
  other arithmetic: 5.54 us -> 0 us
    reduce_scatter x2 -> x0, waiting for transfers between devices: 89 us -> none  [sum_by_axis(): subtotal = lax.psum_scatter(subtotal, axis, scatter_dimension=0, tiled=True)]
    psum x4 -> x0, blocking collectives: 47.1 us -> none  [one_axis_at_a_time(): return functools.reduce(lax.psum, axes, array)]
    pallas_call x0 -> x2, Pallas kernels: none -> 42.5 us  [the longest x1 41.8 us: on_device(): pl.pallas_call(kernel, out_shape=shapes, in_specs=[hbm] * 8, out_specs=[v...]
    dot_general x66 -> x0, matrix products: 38.2 us -> none  [the longest x32 24.6 us: advance(): jnp.dot(hidden, w_out, preferred_element_type=jnp.float32)]
  transfers between devices with their start and end apart: 3 -> 0, of which waited for: 2 -> 0; matrix products, arithmetic and copies ran while one was open for 19% -> 0% of each run, Pallas kernels for 0% -> 0%
where the time goes in v2:
time: 43.2 us; the launch traced here: 43.1 us
  Pallas kernels  42.5 us (98%)
  between operations  0.64 us (1%)
    pallas_call x1, Pallas kernels, on_device(): pl.pallas_call(kernel, out_shape=shapes, in_specs=[hbm] * 8, out_specs=[v...  41.8 us

profile of v2, /device:TPU:1, one launch (start us, length us, event | category | flops | bytes accessed | tf_op | source)
XLA Modules:
  0.0 43.1 jit_solution(6481158981754783693)
XLA Ops:
  0.6 41.8 %shard_map.103 = (f32[1,1024]{1,0:T(1,128)S(1)}, f32[32,1024]{1,0:T(8,128)S(1)}, f32[1,512]{1,0:T(1,128)S(1)}) custom-call(bf16[512,1024]{1,0:T(8,128)(2,1)} %act_hbm.1, s32[1,512]{1,0:T(1,128)} %bitcast.6, f32[1,256]{1,0:T(1,128)} %bitcast.7, bf16[256,256]{1,0:T(8,128)(2,1)} %ws_hbm.1, bf16[32,256]{1,0:T(8,128)(2,1)} %wa_hbm.1, f32[1,256]{1,0:T(1,128)} %bitcast.8, ...), custom_call_target="tpu_custom_call" | custom-call | tf_op jit(solution)/shard_map/pallas_call | solution.py:363
  42.4 0.7 %shard_map.104 = (f32[1,1024]{1,0:T(1,128)}, f32[32,1024]{1,0:T(8,128)}, f32[1,512]{1,0:T(1,128)}) custom-call(f32[1,1024]{1,0:T(1,128)S(1)} %get-tuple-element.9.mean, f32[32,1024]{1,0:T(8,128)S(1)} %get-tuple-element.10.cov, f32[1,512]{1,0:T(1,128)S(1)} %get-tuple-element.11.ret), custom_call_target="tpu_custom_call" | custom-call | tf_op jit(solution)/shard_map/pallas_call | solution.py:371

commit v3 on v2

--- a/solution.py
+++ b/solution.py
@@ -14,7 +14,7 @@
 AXES = ("x", "z", "y", "c")
 NX, NZ, NY = 4, 8, 4
 PACK = 128 // ACT
-FILL = (3, 10, 9, 4, 4, 2)
+FILL = (3, 2, 1, 1, 1, 2, 2, 2, 1, 5, 6, 6)
 
 
 def kernel(
@@ -105,28 +105,29 @@
         ys = b * (1 - core) + a * core
         return copy(part.at[core, xs, ys], own.at[a, b], pair_send.at[a * 4 + b], pair_recv.at[a * 4 + b], {"c": sib})
 
-    def give(a):
-        for b in range(4):
-            cp = pair_copy(sib, a, b)
-            cp.start()
-
     def other(a):
         return a + 1 - 2 * lax.rem(a, 2)
 
+    order = (far2, up2, dn2, pos2)
+    order_sib = (far1, up1, dn1, pos1)
+
+    def give(a):
+        for b in order_sib:
+            pair_copy(sib, a, b).start()
+
+    sums = jnp.dot(jnp.broadcast_to(w_b, (16, w_b.shape[1])), act[...], preferred_element_type=f32)
+    s_c[c, 0:1, :] = sums[0:1]
+    s_c[c, 1:2, :] = jnp.broadcast_to(jnp.sum(w_row, axis=1, keepdims=True), (1, DIM))
     pair_sib = lax.div(far_sib, 2)
     pair_own = lax.div(far1, 2)
     product(sib, pair_sib)
     pl.semaphore_wait(barrier, len(near))
+    sc = copy(s_c.at[c], s_c.at[c], sc_send, sc_recv, {"c": sib})
+    sc.start()
     give(far_sib)
     give(other(far_sib))
     for where in near:
         signal(hello.at[0], where)
-
-    sums = jnp.dot(jnp.broadcast_to(w_b, (16, w_b.shape[1])), act[...], preferred_element_type=f32)
-    s_c[c, 0:1, :] = sums[0:1]
-    s_c[c, 1:2, :] = jnp.broadcast_to(jnp.sum(w_row, axis=1, keepdims=True), (1, DIM))
-    sc = copy(s_c.at[c], s_c.at[c], sc_send, sc_recv, {"c": sib})
-    sc.start()
 
     product(c, pair_own)
     product(sib, 1 - pair_sib)
@@ -143,31 +144,28 @@
     acc[...] = jnp.zeros_like(acc)
     done = 0
 
+    def step(t):
+        block = act[:, pl.ds(pl.multiple_of(lax.div(t, PACK) * 128, 128), 128)]
+        st = state[...]
+        pre = jnp.dot(st.astype(bf16), ws[...], preferred_element_type=f32)
+        pre = pre + jnp.dot(block, wa_pad[lax.rem(t, PACK)], preferred_element_type=f32) + bias[...]
+        hidden = jnp.tanh(pre).astype(bf16)
+        st = 0.9 * st + jnp.dot(hidden, wo[...], preferred_element_type=f32)
+        state[...] = st
+        acc[...] += st
+
     def fill(k):
         nonlocal done
-        count = min(FILL[k], STEPS - done) if k < len(FILL) else STEPS - done
-        if count <= 0:
-            return
-
-        @pl.loop(done, done + count)
-        def _(t):
-            block = act[:, pl.ds(pl.multiple_of(lax.div(t, PACK) * 128, 128), 128)]
-            st = state[...]
-            pre = jnp.dot(st.astype(bf16), ws[...], preferred_element_type=f32)
-            pre = pre + jnp.dot(block, wa_pad[lax.rem(t, PACK)], preferred_element_type=f32) + bias[...]
-            hidden = jnp.tanh(pre).astype(bf16)
-            st = 0.9 * st + jnp.dot(hidden, wo[...], preferred_element_type=f32)
-            state[...] = st
-            acc[...] += st
-
+        count = min(FILL[k], STEPS - done)
+        if count > 0:
+            pl.loop(done, done + count)(step)
         done += count
 
-    def take(a):
-        for b in range(4):
-            pair_copy(c, a, b).wait_recv()
-            xs = a * (1 - c) + b * c
-            ys = b * (1 - c) + a * c
-            own[a, b] = own[a, b] + part[c, xs, ys]
+    def take(a, b):
+        pair_copy(c, a, b).wait_recv()
+        xs = a * (1 - c) + b * c
+        ys = b * (1 - c) + a * c
+        own[a, b] = own[a, b] + part[c, xs, ys]
 
     def all_sum(buf, n):
         total = buf[0]
@@ -192,57 +190,78 @@
     for where in near[3:]:
         signal(hello.at[1], where)
 
-    take(far1)
-    m1p = copy(own.at[far1, :, H0], b1p, r1_send.at[0], r1_recv.at[0], on1(1))
-    m1m = copy(own.at[far1, :, H1], b1m, r1_send.at[1], r1_recv.at[1], on1(3))
-    m1p.start()
-    m1m.start()
+    def ring1(src, a, rows, dst, kind, d):
+        return [
+            copy(src.at[a, b, rows], dst.at[b], r1_send.at[kind, k], r1_recv.at[kind, k], on1(d))
+            for k, b in enumerate(order)
+        ]
+
+    m1p, m1m = ring1(own, far1, H0, b1p, 0, 1), ring1(own, far1, H1, b1m, 1, 3)
+    mdp, mdm = ring1(own, up1, H1, bdp, 2, 1), ring1(own, dn1, H0, bdm, 3, 3)
+    m2p, m2m = ring1(own, up1, H0, b2p, 4, 1), ring1(own, dn1, H1, b2m, 5, 3)
+
+    for k, b in enumerate(order):
+        take(far1, b)
+        m1p[k].start()
+        m1m[k].start()
     fill(0)
-    take(other(far1))
-    take(lax.rem(other(far1) + 2, 4))
-    mdp = copy(own.at[up1, :, H1], bdp, r1_send.at[2], r1_recv.at[2], on1(1))
-    mdm = copy(own.at[dn1, :, H0], bdm, r1_send.at[3], r1_recv.at[3], on1(3))
-    mdp.start()
-    mdm.start()
-    take(pos1)
-
+    for b in order:
+        take(up1, b)
+        take(dn1, b)
+    mdp[0].start()
+    mdm[0].start()
+    for b in order:
+        take(pos1, b)
     fill(1)
 
-    m1p.wait_recv()
-    own[up1, :, H0] = own[up1, :, H0] + b1p[...]
-    m2p = copy(own.at[up1, :, H0], b2p, r1_send.at[4], r1_recv.at[4], on1(1))
-    m2p.start()
-    m1m.wait_recv()
-    own[dn1, :, H1] = own[dn1, :, H1] + b1m[...]
-    m2m = copy(own.at[dn1, :, H1], b2m, r1_send.at[5], r1_recv.at[5], on1(3))
-    m2m.start()
+    for k, b in enumerate(order):
+        m1p[k].wait_recv()
+        own[up1, b, H0] = own[up1, b, H0] + b1p[b]
+        m2p[k].start()
+        m1m[k].wait_recv()
+        own[dn1, b, H1] = own[dn1, b, H1] + b1m[b]
+        m2m[k].start()
+        if k < 3:
+            mdp[k + 1].start()
+            mdm[k + 1].start()
+            fill(2 + k)
 
     pl.semaphore_wait(hello.at[1], 4)
     for where in near[3:]:
         signal(hello.at[2], where)
-    fill(2)
-
     for cp in sx:
         cp.wait_recv()
     s_y[y] = all_sum(s_x, NX)
-
-    mdm.wait_recv()
-    mdp.wait_recv()
-    m2p.wait_recv()
-    mid[:, H0] = own[pos1, :, H0] + b2p[...] + bdm[...]
+    sy = spread(s_y, y, NY, sy_send, sy_recv, at_y)
+    fill(5)
+
+    def low_half(k, b):
+        mdm[k].wait_recv()
+        m2p[k].wait_recv()
+        mid[b, H0] = own[pos1, b, H0] + b2p[b] + bdm[b]
+
+    def high_half(k, b):
+        mdp[k].wait_recv()
+        m2m[k].wait_recv()
+        mid[b, H1] = own[pos1, b, H1] + b2m[b] + bdp[b]
+
+    low_half(0, far2)
     n1p = copy(mid.at[far2, H0], c1p, r2_send.at[0], r2_recv.at[0], on2(1))
     n1p.start()
-    m2m.wait_recv()
-    mid[:, H1] = own[pos1, :, H1] + b2m[...] + bdp[...]
+    high_half(0, far2)
     n1m = copy(mid.at[far2, H1], c1m, r2_send.at[1], r2_recv.at[1], on2(3))
     n1m.start()
-    sy = spread(s_y, y, NY, sy_send, sy_recv, at_y)
+    fill(6)
+    high_half(1, up2)
     ndp = copy(mid.at[up2, H1], cdp, r2_send.at[2], r2_recv.at[2], on2(1))
+    ndp.start()
+    low_half(1, up2)
+    fill(7)
+    low_half(2, dn2)
     ndm = copy(mid.at[dn2, H0], cdm, r2_send.at[3], r2_recv.at[3], on2(3))
-    ndp.start()
     ndm.start()
-
-    fill(3)
+    high_half(2, dn2)
+    fill(8)
 
     n1p.wait_recv()
     mid[up2, H0] = mid[up2, H0] + c1p[...]
@@ -258,8 +277,10 @@
     s_z[z] = all_sum(s_y, NY)
     pl.semaphore_wait(hello.at[2], 4)
     sz = spread(s_z, z, NZ, sz_send, sz_recv, at_z)
-
-    fill(4)
+    low_half(3, pos2)
+    high_half(3, pos2)
+
+    fill(9)
 
     ndm.wait_recv()
     ndp.wait_recv()
@@ -277,7 +298,7 @@
         zs.append(cp)
     zin[z] = low[pl.ds(pl.multiple_of(z * 32, 32), 32), :]
 
-    fill(5)
+    fill(10)
 
     for cp in sz:
         cp.wait_recv()
@@ -300,7 +321,8 @@
         cp.start()
         gs.append(cp)
 
-    fill(6)
+    fill(11)
+    assert done == STEPS
     scaled = acc[...] * (rv[...] * (1.0 / STEPS))
     folded = scaled[:, :128] + scaled[:, 128:]
     ret_ref[...] = jnp.sum(folded.T, axis=0, keepdims=True)
@@ -308,7 +330,7 @@
     for a in range(4):
         for b in range(4):
             pair_copy(sib, a, b).wait_send()
-    for cp in [sc, m1p, m1m, mdp, mdm, m2p, m2m, n1p, n1m, ndp, ndm, n2p, n2m] + sx + sy + sz + zs:
+    for cp in m1p + m1m + mdp + mdm + m2p + m2m + [sc, n1p, n1m, ndp, ndm, n2p, n2m] + sx + sy + sz + zs:
         cp.wait_send()
     for cp in gs:
         cp.wait_recv()
@@ -348,7 +370,7 @@
         + [V((n, 2, DIM), f32) for n in (2, NX, NY, NZ)]
         + [V((PACK, 128, STATE), bf16), V((cand, STATE), f32), V((cand, STATE), f32)]
         + [dma((11,)), pltpu.SemaphoreType.REGULAR((3,))]
-        + [dma((16,)), dma((16,)), dma((6,)), dma((6,)), dma((6,)), dma((6,)), dma((NZ,)), dma((NZ,)), dma((7,)), dma((7,))]
+        + [dma((16,)), dma((16,)), dma((6, 4)), dma((6, 4)), dma((6,)), dma((6,)), dma((NZ,)), dma((NZ,)), dma((7,)), dma((7,))]
         + [dma(()), dma(()), dma((NX,)), dma((NX,)), dma((NY,)), dma((NY,)), dma((NZ,)), dma((NZ,))]
     )
     shapes = (

time: 43.2 us -> 39.5 us (0.914)
  Pallas kernels: 42.5 us -> 38.7 us
    pallas_call x1, Pallas kernels: 41.8 us -> 38.1 us  [on_device(): pl.pallas_call(kernel, out_shape=shapes, in_specs=[hbm] * 8, out_specs=[v...]
where the time goes in v3:
time: 39.5 us; the launch traced here: 39.4 us
  Pallas kernels  38.7 us (98%)
  between operations  0.64 us (2%)
    pallas_call x1, Pallas kernels, on_device(): pl.pallas_call(kernel, out_shape=shapes, in_specs=[hbm] * 8, out_specs=[v...  38.1 us

profile of v3, /device:TPU:1, one launch (start us, length us, event | category | flops | bytes accessed | tf_op | source)
XLA Modules:
  0.0 39.4 jit_solution(4999636778949610611)
XLA Ops:
  0.6 38.1 %shard_map.103 = (f32[1,1024]{1,0:T(1,128)S(1)}, f32[32,1024]{1,0:T(8,128)S(1)}, f32[1,512]{1,0:T(1,128)S(1)}) custom-call(bf16[512,1024]{1,0:T(8,128)(2,1)} %act_hbm.1, s32[1,512]{1,0:T(1,128)} %bitcast.6, f32[1,256]{1,0:T(1,128)} %bitcast.7, bf16[256,256]{1,0:T(8,128)(2,1)} %ws_hbm.1, bf16[32,256]{1,0:T(8,128)(2,1)} %wa_hbm.1, f32[1,256]{1,0:T(1,128)} %bitcast.8, ...), custom_call_target="tpu_custom_call" | custom-call | tf_op jit(solution)/shard_map/pallas_call | solution.py:385
  38.7 0.7 %shard_map.104 = (f32[1,1024]{1,0:T(1,128)}, f32[32,1024]{1,0:T(8,128)}, f32[1,512]{1,0:T(1,128)}) custom-call(f32[1,1024]{1,0:T(1,128)S(1)} %get-tuple-element.9.mean, f32[32,1024]{1,0:T(8,128)S(1)} %get-tuple-element.10.cov, f32[1,512]{1,0:T(1,128)S(1)} %get-tuple-element.11.ret), custom_call_target="tpu_custom_call" | custom-call | tf_op jit(solution)/shard_map/pallas_call | solution.py:393
